TPU v7x, 32 devices: a whole 2x2x4 slice. The times are simulated.
32 devices in a mesh: gx: 2 (over y), gy: 4 (over x, core), gz: 4 (over z).
Axes of the slice: x: 2, y: 2, z: 4, core: 2. Of those that a mesh axis runs over, the one named last changes fastest.
Arguments:
- occupancy: int32 [32, 256, 512], P('gx', 'gy', 'gz'), may hold values 0 or 1
- site_field: float32 [32, 256, 512], P('gx', 'gy', 'gz'), may hold values from -6 to 6
- attempt_rate: float32 [32, 256, 512], P('gx', 'gy', 'gz'), may hold values from 0.2 to 5
- uniforms: float32 [8, 32, 256, 256], P(None, 'gx', 'gy', 'gz'), may hold values from 0.001 to 1
Outputs:
- final_spins: float32 [32, 256, 512], P('gx', 'gy', 'gz')
- history: float32 [2, 8], replicated
All inputs are finite; a program needn't handle non-finite values. No bound on the sum of `occupancy` on one device may be relied on, other than what follows from the above.
Results may differ from a plain program's by a relative error of at most 0.0002.
Values sent between devices are 32-bit elements; how exact they have to be, the bound alone decides.
A program may use at most 128 MiB of HBM per device.

v0:
```python
import jax
import jax.numpy as jnp
from jax import lax
from jax.sharding import PartitionSpec as P

SECTIONS = 8


coupling = 0.5
softness = 0.5


def padded_2(shard, sides, width):
    for axis, dim in sides:
        count, length = (lax.axis_size(axis), shard.shape[dim])
        up = [(i, (i + 1) % count) for i in range(count)]
        down = [(j, i) for i, j in up]
        last = lax.slice_in_dim(shard, length - width, length, axis=dim)
        initial = lax.slice_in_dim(shard, 0, width, axis=dim)
        before = lax.ppermute(last, axis, up)
        after = lax.ppermute(initial, axis, down)
        shard = jnp.concatenate([before, shard, after], axis=dim)
    return shard


def parity_mask(shape, phase):
    xpos = lax.broadcasted_iota(jnp.int32, shape, 0)
    ypos = lax.broadcasted_iota(jnp.int32, shape, 1)
    zpos = lax.broadcasted_iota(jnp.int32, shape, 2)
    return ((xpos + ypos + zpos) % 2 == phase).astype(jnp.float32)


def unpack_draws(packed, phase):
    shape = packed.shape
    xpos = lax.broadcasted_iota(jnp.int32, shape, 0)
    ypos = lax.broadcasted_iota(jnp.int32, shape, 1)
    select = (xpos + ypos + phase) % 2
    first = jnp.where(select == 0, packed, jnp.float32(1.0))
    second = jnp.where(select == 1, packed, jnp.float32(1.0))
    return jnp.stack([first, second], -1).reshape(shape[0], shape[1], 2 * shape[2])


def neighbours(spin):
    padded = padded_2(spin, (("gx", 0), ("gy", 1), ("gz", 2)), 1)
    total = padded[2:, 1:-1, 1:-1] + padded[:-2, 1:-1, 1:-1]
    total = total + padded[1:-1, 2:, 1:-1] + padded[1:-1, :-2, 1:-1]
    return total + padded[1:-1, 1:-1, 2:] + padded[1:-1, 1:-1, :-2]


def body(occupancy, site_field, attempt_rate, uniforms):
    spin = 2.0 * occupancy.astype(jnp.float32) - 1.0
    device_count = lax.axis_size("gx") * lax.axis_size("gy") * lax.axis_size("gz")
    sites_total = spin.size * device_count
    half_sites = sites_total / 2.0
    clock = jnp.float32(0.0)
    energies = []
    times = []
    log_rates = jnp.log(attempt_rate)
    mask = None
    beside_all = None
    for section_index in range(SECTIONS):
        phase = section_index % 2
        mask = parity_mask(spin.shape, phase)
        beside_all = neighbours(spin)
        delta = 2.0 * spin * (site_field - coupling * beside_all)
        rate_log = log_rates - jax.nn.softplus(delta)
        local_rate = jnp.sum(mask * jnp.exp(rate_log))
        total_rate = lax.psum(local_rate, ("gx", "gy", "gz"))
        log_dt = jnp.log(jnp.float32(half_sites)) - jnp.log(total_rate)
        draws_full = unpack_draws(uniforms[section_index], phase)
        accept = jax.nn.sigmoid((rate_log + log_dt - jnp.log(draws_full)) / softness)
        spin = spin - 2.0 * accept * spin * mask
        local_after = coupling * jnp.sum(mask * spin * beside_all) - jnp.sum(site_field * spin)
        energies.append(lax.psum(local_after, ("gx", "gy", "gz")) / sites_total)
        clock = clock + half_sites / total_rate
        times.append(clock)
    history = jnp.stack([jnp.stack(energies), jnp.stack(times)])
    return (spin, history)


def solution(mesh):
    in_specs = (
        P("gx", "gy", "gz"),
        P("gx", "gy", "gz"),
        P("gx", "gy", "gz"),
        P(None, "gx", "gy", "gz"),
    )
    out_specs = (P("gx", "gy", "gz"), P())
    return jax.shard_map(body, mesh=mesh, in_specs=in_specs, out_specs=out_specs, check_vma=False)
```

profile of v0, /device:TPU:0, one launch (start us, length us, event | category | flops | bytes accessed | tf_op | source)
XLA Modules:
  0.0 686.0 jit_solution(13445502910088412051)
XLA Ops:
  2.4 3.1 collective-permute-start.1
  5.5 5.7 bitcast_select_fusion.1
  19.3 3.4 copy.200
  24.6 2.8 copy.196
  28.1 4.0 collective-permute-start.4
  39.4 7.2 %select_reduce_fusion.7 = (f32[]{:T(128)}, f32[16,64,128]{1,0,2:T(8,128)}, f32[16,64,128]{1,0,2:T(8,128)}) fusion(f32[16,64,128]{1,0,2:T(8,128)S(1)} %copy.199, s32[16,64,128]{1,0,2:T(8,128)S(1)} %copy.188, f32[16,64,128]{1,0,2:T(8,128)S(1)} %copy.189, f32[18,66,128]{1,0,2:T(8,128)} %copy.196, f32[18,66,1]{1,0,2:T(8,128)S(1)} %collective-permute-done.5, ...), kind=kLoop, calls=%fused_computation.203 | loop fusion | flops 5111807 | bytes 4877604 | tf_op jit(solution)/shard_map/reduce_sum | solution.py:67
  46.6 40.3 %psum.112 = f32[]{:T(128)} all-reduce(f32[]{:T(128)} %get-tuple-element.54), channel_id=1, replica_groups=mesh['gx'=2,'gy'=4,'gz'=4] {'gx','gy','gz'}, use_global_device_ids=true, to_apply=%region_1.2 | all-reduce | flops 1 | bytes 8 | tf_op jit(solution)/shard_map/psum | solution.py:68
  112.6 6.0 select_reduce_fusion.6
  118.6 39.8 %psum.113 = f32[]{:T(128)} all-reduce(f32[]{:T(128)} %get-tuple-element.51), channel_id=1, replica_groups=mesh['gx'=2,'gy'=4,'gz'=4] {'gx','gy','gz'}, use_global_device_ids=true, to_apply=%region_3.4 | all-reduce | flops 1 | bytes 8 | tf_op jit(solution)/shard_map/psum | solution.py:68
  172.2 3.0 copy.222
  176.2 2.8 copy.218
  187.9 7.1 %select_reduce_fusion.5 = (f32[]{:T(128)}, f32[16,64,128]{1,0,2:T(8,128)}, f32[16,64,128]{1,0,2:T(8,128)}) fusion(f32[16,64,128]{1,0,2:T(8,128)} %copy-done, f32[16,64,128]{1,0,2:T(8,128)S(1)} %fusion.111, f32[16,64,128]{1,0,2:T(8,128)} %copy-done.2, f32[18,66,128]{1,0,2:T(8,128)} %copy.218, f32[18,66,1]{1,0,2:T(8,128)S(1)} %collective-permute-done.17, ...), kind=kLoop, calls=%fused_computation.201 | loop fusion | flops 4718591 | bytes 4353316 | tf_op jit(solution)/shard_map/reduce_sum | solution.py:67
  195.0 39.3 %psum.114 = f32[]{:T(128)} all-reduce(f32[]{:T(128)} %get-tuple-element.48), channel_id=1, replica_groups=mesh['gx'=2,'gy'=4,'gz'=4] {'gx','gy','gz'}, use_global_device_ids=true, to_apply=%region_5.6 | all-reduce | flops 1 | bytes 8 | tf_op jit(solution)/shard_map/psum | solution.py:68
  248.3 3.0 copy.233
  252.2 2.8 copy.229
  263.8 7.1 %select_reduce_fusion.4 = (f32[]{:T(128)}, f32[16,64,128]{1,0,2:T(8,128)}, f32[16,64,128]{1,0,2:T(8,128)}) fusion(f32[16,64,128]{1,0,2:T(8,128)} %copy-done, f32[16,64,128]{1,0,2:T(8,128)S(1)} %fusion.102, f32[16,64,128]{1,0,2:T(8,128)} %copy-done.2, f32[18,66,128]{1,0,2:T(8,128)} %copy.229, f32[18,66,1]{1,0,2:T(8,128)S(1)} %collective-permute-done.23, ...), kind=kLoop, calls=%fused_computation.200 | loop fusion | flops 4718591 | bytes 4353316 | tf_op jit(solution)/shard_map/reduce_sum | solution.py:67
  270.9 39.9 %psum.115 = f32[]{:T(128)} all-reduce(f32[]{:T(128)} %get-tuple-element.45), channel_id=1, replica_groups=mesh['gx'=2,'gy'=4,'gz'=4] {'gx','gy','gz'}, use_global_device_ids=true, to_apply=%region_7.8 | all-reduce | flops 1 | bytes 8 | tf_op jit(solution)/shard_map/psum | solution.py:68
  324.6 3.0 copy.244
  328.5 2.8 copy.240
  340.4 7.1 %select_reduce_fusion.3 = (f32[]{:T(128)}, f32[16,64,128]{1,0,2:T(8,128)}, f32[16,64,128]{1,0,2:T(8,128)}) fusion(f32[16,64,128]{1,0,2:T(8,128)} %copy-done, f32[16,64,128]{1,0,2:T(8,128)S(1)} %fusion.93, f32[16,64,128]{1,0,2:T(8,128)} %copy-done.2, f32[18,66,128]{1,0,2:T(8,128)} %copy.240, f32[18,66,1]{1,0,2:T(8,128)S(1)} %collective-permute-done.29, ...), kind=kLoop, calls=%fused_computation.199 | loop fusion | flops 4718591 | bytes 4353316 | tf_op jit(solution)/shard_map/reduce_sum | solution.py:67
  347.4 39.7 %psum.116 = f32[]{:T(128)} all-reduce(f32[]{:T(128)} %get-tuple-element.42), channel_id=1, replica_groups=mesh['gx'=2,'gy'=4,'gz'=4] {'gx','gy','gz'}, use_global_device_ids=true, to_apply=%region_9.10 | all-reduce | flops 1 | bytes 8 | tf_op jit(solution)/shard_map/psum | solution.py:68
  401.0 3.1 copy.255
  416.6 7.1 %select_reduce_fusion.2 = (f32[]{:T(128)}, f32[16,64,128]{1,0,2:T(8,128)}, f32[16,64,128]{1,0,2:T(8,128)}) fusion(f32[16,64,128]{1,0,2:T(8,128)} %copy-done, f32[16,64,128]{1,0,2:T(8,128)S(1)} %fusion.84, f32[16,64,128]{1,0,2:T(8,128)} %copy-done.2, f32[18,66,128]{1,0,2:T(8,128)} %copy.251, f32[18,66,1]{1,0,2:T(8,128)S(1)} %collective-permute-done.35, ...), kind=kLoop, calls=%fused_computation.198 | loop fusion | flops 4718591 | bytes 4353316 | tf_op jit(solution)/shard_map/reduce_sum | solution.py:67
  423.7 39.8 %psum.117 = f32[]{:T(128)} all-reduce(f32[]{:T(128)} %get-tuple-element.39), channel_id=1, replica_groups=mesh['gx'=2,'gy'=4,'gz'=4] {'gx','gy','gz'}, use_global_device_ids=true, to_apply=%region_11.12 | all-reduce | flops 1 | bytes 8 | tf_op jit(solution)/shard_map/psum | solution.py:68
  477.2 3.0 copy.266
  493.0 7.0 %select_reduce_fusion.1 = (f32[]{:T(128)}, f32[16,64,128]{1,0,2:T(8,128)}, f32[16,64,128]{1,0,2:T(8,128)}) fusion(f32[16,64,128]{1,0,2:T(8,128)} %copy-done, f32[16,64,128]{1,0,2:T(8,128)S(1)} %fusion.75, f32[16,64,128]{1,0,2:T(8,128)} %copy-done.2, f32[18,66,128]{1,0,2:T(8,128)} %copy.262, f32[18,66,1]{1,0,2:T(8,128)S(1)} %collective-permute-done.41, ...), kind=kLoop, calls=%fused_computation.197 | loop fusion | flops 4718591 | bytes 4353316 | tf_op jit(solution)/shard_map/reduce_sum | solution.py:67
  500.1 39.3 %psum.118 = f32[]{:T(128)} all-reduce(f32[]{:T(128)} %get-tuple-element.36), channel_id=1, replica_groups=mesh['gx'=2,'gy'=4,'gz'=4] {'gx','gy','gz'}, use_global_device_ids=true, to_apply=%region_13.14 | all-reduce | flops 1 | bytes 8 | tf_op jit(solution)/shard_map/psum | solution.py:68
  553.2 3.0 copy.277
  571.8 7.4 %select_reduce_fusion = (f32[]{:T(128)}, f32[16,64,128]{1,0,2:T(8,128)}, f32[16,64,128]{1,0,2:T(8,128)}) fusion(f32[16,64,128]{1,0,2:T(8,128)S(1)} %copy-done.1, f32[16,64,128]{1,0,2:T(8,128)} %copy-done.9, f32[16,64,128]{1,0,2:T(8,128)S(1)} %copy-done.3, f32[18,66,128]{1,0,2:T(8,128)} %copy-done.12, f32[18,66,1]{1,0,2:T(8,128)S(1)} %collective-permute-done.47, ...), kind=kLoop, calls=%fused_computation.196 | loop fusion | flops 4718591 | bytes 4353316 | tf_op jit(solution)/shard_map/reduce_sum | solution.py:67
  579.3 40.0 %psum.119 = f32[]{:T(128)} all-reduce(f32[]{:T(128)} %get-tuple-element.33), channel_id=1, replica_groups=mesh['gx'=2,'gy'=4,'gz'=4] {'gx','gy','gz'}, use_global_device_ids=true, to_apply=%region_15.16 | all-reduce | flops 1 | bytes 8 | tf_op jit(solution)/shard_map/psum | solution.py:68
  620.7 8.0 %multiply_reduce_fusion = (f32[]{:T(128)}, f32[]{:T(128)}, f32[]{:T(128)}, f32[]{:T(128)}, f32[]{:T(128)}, /*index=5*/f32[]{:T(128)}, f32[]{:T(128)}, f32[]{:T(1...) fusion(f32[16,64,128]{1,0,2:T(8,128)S(1)} %copy-done.1, ...), kind=kLoop, calls=%fused_computation.180 | loop fusion | flops 8519664 | bytes 9961540 | tf_op jit(solution)/shard_map/reduce_sum | solution.py:73
  639.9 40.1 %all-reduce = (f32[]{:T(128)}, f32[]{:T(128)}, f32[]{:T(128)}, f32[]{:T(128)}, f32[]{:T(128)}, /*index=5*/f32[]{:T(128)}, f32[]{:T(128)}, f32[]{:T(128)}) all-reduce(f32[]{:T(128)S(6)} %sub.188, f32[]{:T(128)S(6)} %sub.189, f32[]{:T(128)S(6)} %sub.190, f32[]{:T(128)S(6)} %sub.191, ...), channel_id=1, replica_groups=mesh['gx'=2,'gy'=4,'gz'=4] {'gx','gy','gz'}, use_global_device_ids=true, to_apply=%region_18.19 | all-reduce | flops 8 | bytes 64 | tf_op jit(solution)/shard_map/psum | solution.py:74
  (242 shorter events, 191.4 us)
Async XLA Ops:
  2.4 9.2 %collective-permute-start.1 = (f32[1,64,128]{1,0,2:T(1,128)S(1)}, f32[1,64,128]{1,0,2:T(1,128)S(1)}, u32[]{:S(2)}, u32[]{:S(2)}) collective-permute-start(f32[1,64,128]{1,0,2:T(1,128)S(1)} %get-tuple-element.103), channel_id=1, source_target_pairs={{0,16},{16,0},{1,17},{17,1},{2,18},{18,2},{3,19},{19,3},{4,20},{20... | collective-permute-start | bytes 98312 | tf_op jit(solution)/shard_map/ppermute | solution.py:20
  5.5 6.3 collective-permute-start
  11.8 10.8 %collective-permute-start.3 = (f32[18,1,128]{2,1,0:T(1,128)S(1)}, f32[18,1,128]{2,1,0:T(1,128)S(1)}, u32[]{:S(2)}, u32[]{:S(2)}) collective-permute-start(f32[18,1,128]{2,1,0:T(1,128)S(1)} %get-tuple-element.135), channel_id=1, source_target_pairs={{0,4},{4,8},{8,12},{12,0},{1,5},{5,9},{9,13},{13,1},{2,6},{6,10},{... | collective-permute-start | bytes 27656 | tf_op jit(solution)/shard_map/ppermute | solution.py:20
  11.9 10.8 %collective-permute-start.2 = (f32[18,1,128]{2,1,0:T(1,128)S(1)}, f32[18,1,128]{2,1,0:T(1,128)S(1)}, u32[]{:S(2)}, u32[]{:S(2)}) collective-permute-start(f32[18,1,128]{2,1,0:T(1,128)S(1)} %get-tuple-element.136), channel_id=1, source_target_pairs={{4,0},{8,4},{12,8},{0,12},{5,1},{9,5},{13,9},{1,13},{6,2},{10,6},{... | collective-permute-start | bytes 27656 | tf_op jit(solution)/shard_map/ppermute | solution.py:21
  28.1 11.3 %collective-permute-start.4 = (f32[18,66,1]{1,0,2:T(8,128)S(1)}, f32[18,66,1]{1,0,2:T(8,128)S(1)}, u32[]{:S(2)}, u32[]{:S(2)}) collective-permute-start(f32[18,66,1]{1,0,2:T(8,128)S(1)} %get-tuple-element.87), channel_id=1, source_target_pairs={{1,0},{2,1},{3,2},{0,3},{5,4},{6,5},{7,6},{4,7},{9,8},{10,9},{11,1... | collective-permute-start | bytes 14264 | tf_op jit(solution)/shard_map/ppermute | solution.py:21
  32.1 7.3 %collective-permute-start.5 = (f32[18,66,1]{1,0,2:T(8,128)S(1)}, f32[18,66,1]{1,0,2:T(8,128)S(1)}, u32[]{:S(2)}, u32[]{:S(2)}) collective-permute-start(f32[18,66,1]{1,0,2:T(8,128)S(1)} %get-tuple-element.88), channel_id=1, source_target_pairs={{0,1},{1,2},{2,3},{3,0},{4,5},{5,6},{6,7},{7,4},{8,9},{9,10},{10,1... | collective-permute-start | bytes 14264 | tf_op jit(solution)/shard_map/ppermute | solution.py:20
  104.2 8.4 %collective-permute-start.10 = (f32[18,66,1]{1,0,2:T(8,128)S(1)}, f32[18,66,1]{1,0,2:T(8,128)S(1)}, u32[]{:S(2)}, u32[]{:S(2)}) collective-permute-start(f32[18,66,1]{1,0,2:T(8,128)S(1)} %get-tuple-element.85), channel_id=1, source_target_pairs={{1,0},{2,1},{3,2},{0,3},{5,4},{6,5},{7,6},{4,7},{9,8},{10,9},{11,1... | collective-permute-start | bytes 14264 | tf_op jit(solution)/shard_map/ppermute | solution.py:21
  105.8 6.8 collective-permute-start.11
  168.3 7.0 %collective-permute-start.15 = (f32[18,1,128]{2,1,0:T(1,128)S(1)}, f32[18,1,128]{2,1,0:T(1,128)S(1)}, u32[]{:S(2)}, u32[]{:S(2)}) collective-permute-start(f32[18,1,128]{2,1,0:T(1,128)S(1)} %get-tuple-element.127), channel_id=1, source_target_pairs={{0,4},{4,8},{8,12},{12,0},{1,5},{5,9},{9,13},{13,1},{2,6},{6,10},{... | collective-permute-start | bytes 27656 | tf_op jit(solution)/shard_map/ppermute | solution.py:20
  168.3 6.9 %collective-permute-start.14 = (f32[18,1,128]{2,1,0:T(1,128)S(1)}, f32[18,1,128]{2,1,0:T(1,128)S(1)}, u32[]{:S(2)}, u32[]{:S(2)}) collective-permute-start(f32[18,1,128]{2,1,0:T(1,128)S(1)} %get-tuple-element.128), channel_id=1, source_target_pairs={{4,0},{8,4},{12,8},{0,12},{5,1},{9,5},{13,9},{1,13},{6,2},{10,6},{... | collective-permute-start | bytes 27656 | tf_op jit(solution)/shard_map/ppermute | solution.py:21
  179.7 8.3 %collective-permute-start.16 = (f32[18,66,1]{1,0,2:T(8,128)S(1)}, f32[18,66,1]{1,0,2:T(8,128)S(1)}, u32[]{:S(2)}, u32[]{:S(2)}) collective-permute-start(f32[18,66,1]{1,0,2:T(8,128)S(1)} %get-tuple-element.83), channel_id=1, source_target_pairs={{1,0},{2,1},{3,2},{0,3},{5,4},{6,5},{7,6},{4,7},{9,8},{10,9},{11,1... | collective-permute-start | bytes 14264 | tf_op jit(solution)/shard_map/ppermute | solution.py:21
  181.9 6.0 collective-permute-start.17
  244.2 7.2 %collective-permute-start.21 = (f32[18,1,128]{2,1,0:T(1,128)S(1)}, f32[18,1,128]{2,1,0:T(1,128)S(1)}, u32[]{:S(2)}, u32[]{:S(2)}) collective-permute-start(f32[18,1,128]{2,1,0:T(1,128)S(1)} %get-tuple-element.123), channel_id=1, source_target_pairs={{0,4},{4,8},{8,12},{12,0},{1,5},{5,9},{9,13},{13,1},{2,6},{6,10},{... | collective-permute-start | bytes 27656 | tf_op jit(solution)/shard_map/ppermute | solution.py:20
  244.2 7.1 %collective-permute-start.20 = (f32[18,1,128]{2,1,0:T(1,128)S(1)}, f32[18,1,128]{2,1,0:T(1,128)S(1)}, u32[]{:S(2)}, u32[]{:S(2)}) collective-permute-start(f32[18,1,128]{2,1,0:T(1,128)S(1)} %get-tuple-element.124), channel_id=1, source_target_pairs={{4,0},{8,4},{12,8},{0,12},{5,1},{9,5},{13,9},{1,13},{6,2},{10,6},{... | collective-permute-start | bytes 27656 | tf_op jit(solution)/shard_map/ppermute | solution.py:21
  255.7 8.1 %collective-permute-start.22 = (f32[18,66,1]{1,0,2:T(8,128)S(1)}, f32[18,66,1]{1,0,2:T(8,128)S(1)}, u32[]{:S(2)}, u32[]{:S(2)}) collective-permute-start(f32[18,66,1]{1,0,2:T(8,128)S(1)} %get-tuple-element.81), channel_id=1, source_target_pairs={{1,0},{2,1},{3,2},{0,3},{5,4},{6,5},{7,6},{4,7},{9,8},{10,9},{11,1... | collective-permute-start | bytes 14264 | tf_op jit(solution)/shard_map/ppermute | solution.py:21
  257.3 6.5 collective-permute-start.23
  320.6 6.9 %collective-permute-start.27 = (f32[18,1,128]{2,1,0:T(1,128)S(1)}, f32[18,1,128]{2,1,0:T(1,128)S(1)}, u32[]{:S(2)}, u32[]{:S(2)}) collective-permute-start(f32[18,1,128]{2,1,0:T(1,128)S(1)} %get-tuple-element.119), channel_id=1, source_target_pairs={{0,4},{4,8},{8,12},{12,0},{1,5},{5,9},{9,13},{13,1},{2,6},{6,10},{... | collective-permute-start | bytes 27656 | tf_op jit(solution)/shard_map/ppermute | solution.py:20
  320.7 6.9 %collective-permute-start.26 = (f32[18,1,128]{2,1,0:T(1,128)S(1)}, f32[18,1,128]{2,1,0:T(1,128)S(1)}, u32[]{:S(2)}, u32[]{:S(2)}) collective-permute-start(f32[18,1,128]{2,1,0:T(1,128)S(1)} %get-tuple-element.120), channel_id=1, source_target_pairs={{4,0},{8,4},{12,8},{0,12},{5,1},{9,5},{13,9},{1,13},{6,2},{10,6},{... | collective-permute-start | bytes 27656 | tf_op jit(solution)/shard_map/ppermute | solution.py:21
  332.0 8.3 %collective-permute-start.28 = (f32[18,66,1]{1,0,2:T(8,128)S(1)}, f32[18,66,1]{1,0,2:T(8,128)S(1)}, u32[]{:S(2)}, u32[]{:S(2)}) collective-permute-start(f32[18,66,1]{1,0,2:T(8,128)S(1)} %get-tuple-element.79), channel_id=1, source_target_pairs={{1,0},{2,1},{3,2},{0,3},{5,4},{6,5},{7,6},{4,7},{9,8},{10,9},{11,1... | collective-permute-start | bytes 14264 | tf_op jit(solution)/shard_map/ppermute | solution.py:21
  334.3 6.1 collective-permute-start.29
  397.0 7.0 %collective-permute-start.33 = (f32[18,1,128]{2,1,0:T(1,128)S(1)}, f32[18,1,128]{2,1,0:T(1,128)S(1)}, u32[]{:S(2)}, u32[]{:S(2)}) collective-permute-start(f32[18,1,128]{2,1,0:T(1,128)S(1)} %get-tuple-element.115), channel_id=1, source_target_pairs={{0,4},{4,8},{8,12},{12,0},{1,5},{5,9},{9,13},{13,1},{2,6},{6,10},{... | collective-permute-start | bytes 27656 | tf_op jit(solution)/shard_map/ppermute | solution.py:20
  397.1 7.0 %collective-permute-start.32 = (f32[18,1,128]{2,1,0:T(1,128)S(1)}, f32[18,1,128]{2,1,0:T(1,128)S(1)}, u32[]{:S(2)}, u32[]{:S(2)}) collective-permute-start(f32[18,1,128]{2,1,0:T(1,128)S(1)} %get-tuple-element.116), channel_id=1, source_target_pairs={{4,0},{8,4},{12,8},{0,12},{5,1},{9,5},{13,9},{1,13},{6,2},{10,6},{... | collective-permute-start | bytes 27656 | tf_op jit(solution)/shard_map/ppermute | solution.py:21
  408.5 8.2 %collective-permute-start.34 = (f32[18,66,1]{1,0,2:T(8,128)S(1)}, f32[18,66,1]{1,0,2:T(8,128)S(1)}, u32[]{:S(2)}, u32[]{:S(2)}) collective-permute-start(f32[18,66,1]{1,0,2:T(8,128)S(1)} %get-tuple-element.77), channel_id=1, source_target_pairs={{1,0},{2,1},{3,2},{0,3},{5,4},{6,5},{7,6},{4,7},{9,8},{10,9},{11,1... | collective-permute-start | bytes 14264 | tf_op jit(solution)/shard_map/ppermute | solution.py:21
  410.1 6.6 collective-permute-start.35
  473.3 6.9 %collective-permute-start.39 = (f32[18,1,128]{2,1,0:T(1,128)S(1)}, f32[18,1,128]{2,1,0:T(1,128)S(1)}, u32[]{:S(2)}, u32[]{:S(2)}) collective-permute-start(f32[18,1,128]{2,1,0:T(1,128)S(1)} %get-tuple-element.111), channel_id=1, source_target_pairs={{0,4},{4,8},{8,12},{12,0},{1,5},{5,9},{9,13},{13,1},{2,6},{6,10},{... | collective-permute-start | bytes 27656 | tf_op jit(solution)/shard_map/ppermute | solution.py:20
  473.4 6.9 %collective-permute-start.38 = (f32[18,1,128]{2,1,0:T(1,128)S(1)}, f32[18,1,128]{2,1,0:T(1,128)S(1)}, u32[]{:S(2)}, u32[]{:S(2)}) collective-permute-start(f32[18,1,128]{2,1,0:T(1,128)S(1)} %get-tuple-element.112), channel_id=1, source_target_pairs={{4,0},{8,4},{12,8},{0,12},{5,1},{9,5},{13,9},{1,13},{6,2},{10,6},{... | collective-permute-start | bytes 27656 | tf_op jit(solution)/shard_map/ppermute | solution.py:21
  484.7 8.4 %collective-permute-start.40 = (f32[18,66,1]{1,0,2:T(8,128)S(1)}, f32[18,66,1]{1,0,2:T(8,128)S(1)}, u32[]{:S(2)}, u32[]{:S(2)}) collective-permute-start(f32[18,66,1]{1,0,2:T(8,128)S(1)} %get-tuple-element.75), channel_id=1, source_target_pairs={{1,0},{2,1},{3,2},{0,3},{5,4},{6,5},{7,6},{4,7},{9,8},{10,9},{11,1... | collective-permute-start | bytes 14264 | tf_op jit(solution)/shard_map/ppermute | solution.py:21
  486.9 6.1 collective-permute-start.41
  549.2 11.7 %collective-permute-start.45 = (f32[18,1,128]{2,1,0:T(1,128)S(1)}, f32[18,1,128]{2,1,0:T(1,128)S(1)}, u32[]{:S(2)}, u32[]{:S(2)}) collective-permute-start(f32[18,1,128]{2,1,0:T(1,128)S(1)} %get-tuple-element.107), channel_id=1, source_target_pairs={{0,4},{4,8},{8,12},{12,0},{1,5},{5,9},{9,13},{13,1},{2,6},{6,10},{... | collective-permute-start | bytes 27656 | tf_op jit(solution)/shard_map/ppermute | solution.py:20
  549.3 11.6 %collective-permute-start.44 = (f32[18,1,128]{2,1,0:T(1,128)S(1)}, f32[18,1,128]{2,1,0:T(1,128)S(1)}, u32[]{:S(2)}, u32[]{:S(2)}) collective-permute-start(f32[18,1,128]{2,1,0:T(1,128)S(1)} %get-tuple-element.108), channel_id=1, source_target_pairs={{4,0},{8,4},{12,8},{0,12},{5,1},{9,5},{13,9},{1,13},{6,2},{10,6},{... | collective-permute-start | bytes 27656 | tf_op jit(solution)/shard_map/ppermute | solution.py:21
  563.5 8.3 %collective-permute-start.46 = (f32[18,66,1]{1,0,2:T(8,128)S(1)}, f32[18,66,1]{1,0,2:T(8,128)S(1)}, u32[]{:S(2)}, u32[]{:S(2)}) collective-permute-start(f32[18,66,1]{1,0,2:T(8,128)S(1)} %get-tuple-element.73), channel_id=1, source_target_pairs={{1,0},{2,1},{3,2},{0,3},{5,4},{6,5},{7,6},{4,7},{9,8},{10,9},{11,1... | collective-permute-start | bytes 14264 | tf_op jit(solution)/shard_map/ppermute | solution.py:21
  565.2 6.7 collective-permute-start.47
  (36 other events, 565.9 us)
where the time goes:
time: 698 us; the launch traced here: 686 us
  blocking collectives  358 us (51%)
  other arithmetic  120 us (17%)
  local copies, waits for them, and re-layouts  98 us (14%)
  starting transfers between devices  56.1 us (8%)
  between operations  27.3 us (4%)
  waiting for transfers between devices  26 us (4%)
    psum x8, blocking collectives, body(): total_rate = lax.psum(local_rate, ('gx', 'gy', 'gz'))  318 us
    reduce_sum x8, other arithmetic, body(): local_rate = jnp.sum(mask * jnp.exp(rate_log))  56 us
    unnamed x60, local copies, waits for them, and re-layouts  45.3 us
    psum x1, blocking collectives, body(): energies.append(lax.psum(local_after, ('gx', 'gy', 'gz')) / sites_total)  40.1 us
    ppermute x24, starting transfers between devices, padded_2(): after = lax.ppermute(initial, axis, down)  32 us
    ppermute x24, starting transfers between devices, padded_2(): before = lax.ppermute(last, axis, up)  24.2 us
    log x8, local copies, waits for them, and re-layouts, body(): jnp.log(draws_full)  23.1 us
    concatenate x8, local copies, waits for them, and re-layouts, padded_2(): shard = jnp.concatenate([before, shard, after], axis=dim)  19.8 us
  transfers between devices with their start and end apart: 48, of which 14 were waited for; matrix products, arithmetic and copies ran while one was open for 15% of the time, Pallas kernels for 0%

commit v1 on v0

v1 whole, which is shorter than its diff:
```python
import functools
import itertools

import jax
import jax.numpy as jnp
from jax import lax
from jax.experimental import pallas as pl
from jax.experimental.pallas import tpu as pltpu
from jax.sharding import PartitionSpec as P

SECTIONS = 8
AXES = ("gx", "gy", "gz")
MESH = pl.DeviceIdType.MESH
PAD = 8


def kernel(sizes, occ, fld, att, uni, out, hist, spin, field, rate0, inv, draw, ratio, local, ghost, hsend, hrecv,
           rsend, rrecv, hs, hr, rs, rr):
    gx, gy, gz = sizes
    count = gx * gy * gz
    planes, rows, lanes = ratio.shape
    half = lanes // 2
    tiles = rows // 8
    body = pl.ds(PAD, rows)
    xdirs = 1 if gx == 2 else 2
    ybase, zbase = tiles * xdirs, tiles * xdirs + 2
    half_sites = float(planes * rows * lanes * count)
    pos = [lax.axis_index(axis) for axis in AXES]
    me = (pos[0] * gy + pos[1]) * gz + pos[2]
    moved = [[lax.rem(pos[a] + d, sizes[a]) for d in range(sizes[a])] for a in range(3)]

    def device(dx, dy, dz):
        return (moved[0][dx % gx], moved[1][dy % gy], moved[2][dz % gz])

    others = [o for o in itertools.product(range(gx), range(gy), range(gz)) if o != (0, 0, 0)]
    others.sort(key=lambda o: -(min(o[0], gx - o[0]) + min(o[1], gy - o[1]) + 2 * min(o[2], gz - o[2])))

    barrier = pltpu.get_barrier_semaphore()
    for o in others:
        pl.semaphore_signal(barrier, inc=1, device_id=device(*o), device_id_type=MESH)

    lane = lax.broadcasted_iota(jnp.int32, (rows, lanes), 1)
    row = lax.broadcasted_iota(jnp.int32, (rows, lanes), 0)
    low = lane < half
    place = lax.rem(lane, half)
    last = place == half - 1
    even = (row & 1) == 0
    odd = (row & 1) == 1
    lane8 = lax.broadcasted_iota(jnp.int32, (8, lanes), 1)
    row8 = lax.broadcasted_iota(jnp.int32, (8, lanes), 0)

    def kind(parity):
        return even if parity % 2 == 0 else odd

    def turn(x, shift):
        return pltpu.roll(x, shift % lanes, 1)

    zrow = lax.broadcasted_iota(jnp.int32, (lanes, lanes), 0)
    zcol = lax.broadcasted_iota(jnp.int32, (lanes, lanes), 1)
    split = (zrow == 2 * lax.rem(zcol, half) + zcol // half).astype(jnp.float32)
    join = (zcol == 2 * lax.rem(zrow, half) + zrow // half).astype(jnp.float32)

    def exact(a, b):
        return jnp.dot(a, b, precision=lax.Precision.HIGHEST, preferred_element_type=jnp.float32)

    def packed(ref, xi):
        first = exact(ref[xi].astype(jnp.float32), split)
        second = exact(ref[xi + planes].astype(jnp.float32), split)
        evens = jnp.where(low, first, turn(second, half))
        odds = jnp.where(low, turn(first, half), second)
        flip = ((row + xi) & 1) == 1
        return jnp.where(flip, odds, evens), jnp.where(flip, evens, odds)

    def prepare(xi, sums):
        s = packed(occ, xi)
        f = packed(fld, xi)
        a = packed(att, xi)
        for p in range(2):
            spin[p, xi + 1, body, :] = 2.0 * s[p] - 1.0
            field[p, xi] = f[p]
            rate0[p, xi] = a[p]
            inv[p, xi] = 1.0 / a[p]
        return sums + fold(f[1] * (2.0 * s[1] - 1.0))

    def fold(x):
        return jnp.sum(x.reshape(tiles, 8, lanes), axis=0)

    zero = jnp.zeros((8, lanes), jnp.float32)
    field_sum = lax.fori_loop(0, planes, prepare, zero)

    def set_draws(k, p):
        for xi in range(planes):
            both = jnp.concatenate([uni[k, xi], uni[k, xi + planes]], axis=1)
            draw[xi] = both * inv[p, xi]

    def halo_copies(slot):
        src = hsend.at[slot]
        up_x, down_x = device(1, 0, 0), device(-1, 0, 0)
        dst = hrecv.at[slot]
        moves = []
        if xdirs == 1:
            moves.append((pl.ds(0, tiles), pl.ds(0, tiles), up_x))
        else:
            moves.append((pl.ds(0, tiles), pl.ds(0, tiles), down_x))
            moves.append((pl.ds(0, tiles), pl.ds(tiles, tiles), up_x))
        moves.append((pl.ds(tiles, 1), pl.ds(ybase, 1), device(0, -1, 0)))
        moves.append((pl.ds(tiles + 1, 1), pl.ds(ybase + 1, 1), device(0, 1, 0)))
        moves.append((pl.ds(tiles + 2, 1), pl.ds(zbase, 1), device(0, 0, 1)))
        moves.append((pl.ds(tiles + 2, 1), pl.ds(zbase + 1, 1), device(0, 0, -1)))
        for a, b, target in moves:
            pltpu.make_async_remote_copy(src.at[a], dst.at[b], hs.at[slot], hr.at[slot], device_id=target, device_id_type=MESH).start()

    def send_halo(slot, plane, user):
        hsend[slot, pl.ds(0, tiles)] = jnp.where(low, plane(0), plane(planes - 1)).reshape(tiles, 8, lanes)
        tail = jnp.zeros((rows, lanes), jnp.float32)
        for xi in range(planes):
            full = plane(xi)
            hsend[slot, tiles, pl.ds(xi, 1), :] = full[0:1]
            hsend[slot, tiles + 1, pl.ds(xi, 1), :] = full[rows - 1:rows]
            ends = jnp.where(kind(xi + user), full, turn(full, -1))
            tail = tail + jnp.where(place == half - 1 - xi, turn(ends, -xi), 0.0)
        z = tail[0:8]
        for t in range(1, tiles):
            z = z + turn(tail[8 * t:8 * t + 8], -planes * t)
        hsend[slot, tiles + 2] = z
        halo_copies(slot)

    def wait_halo(slot):
        whole = hrecv.at[slot]
        pltpu.make_async_copy(whole, whole, hr.at[slot]).wait()
        pltpu.make_async_copy(whole, whole, hs.at[slot]).wait()

    def received(slot, user):
        xs = hrecv[slot, pl.ds(0, tiles)].reshape(rows, lanes)
        if xdirs == 2:
            xs = jnp.where(low, xs, hrecv[slot, pl.ds(tiles, tiles)].reshape(rows, lanes))
        ys = (hrecv[slot, ybase], hrecv[slot, ybase + 1])
        down = ((lane8 + 1 + row8 + user) & 1) == 0
        return xs, ys, jnp.where(down, hrecv[slot, zbase], hrecv[slot, zbase + 1])

    def store_ghosts(p, xs, ys, zs):
        ghost[p, pl.ds(0, tiles)] = xs.reshape(tiles, 8, lanes)
        ghost[p, tiles], ghost[p, tiles + 1] = ys
        ghost[p, tiles + 2] = zs

    def load_ghosts(p):
        return ghost[p, pl.ds(0, tiles)].reshape(rows, lanes), (ghost[p, tiles], ghost[p, tiles + 1]), ghost[p, tiles + 2]

    def place_ghosts(p):
        xs, (above, below), _ = load_ghosts(p)
        spin[p, 0, body, :] = turn(jnp.where(low, spin[p, planes, body, :], xs), half)
        spin[p, planes + 1, body, :] = turn(jnp.where(low, xs, spin[p, 1, body, :]), half)
        for xi in range(planes):
            spin[p, xi + 1, pl.ds(PAD - 1, 1), :] = below[xi:xi + 1]
            spin[p, xi + 1, pl.ds(PAD + rows, 1), :] = above[xi:xi + 1]

    def rates(q):
        p = 1 - q
        zs = ghost[p, tiles + 2]
        ztile = jnp.concatenate([turn(zs, planes * t + half) for t in range(tiles)], axis=0)
        total = zero
        for xi in range(planes):
            mid = spin[p, xi + 1, body, :]
            edge = turn(ztile, xi)
            before = turn(jnp.where(last, edge, mid), 1)
            after = jnp.where(last, edge, turn(mid, -1))
            beside = spin[p, xi, body, :] + spin[p, xi + 2, body, :]
            beside = beside + spin[p, xi + 1, pl.ds(PAD - 1, rows), :] + spin[p, xi + 1, pl.ds(PAD + 1, rows), :]
            beside = beside + mid + jnp.where(kind(xi + q), before, after)
            h = field[q, xi] - 0.5 * beside
            grown = 1.0 + jnp.exp(2.0 * spin[q, xi + 1, body, :] * h)
            r = draw[xi] * grown
            ratio[xi] = r * r
            local[xi] = h
            total = total + fold(rate0[q, xi] / grown)
        return total

    def send_rates(slot, rate, energy):
        both = jnp.where(lane8 < half, rate + turn(rate, half), energy + turn(energy, half))
        message = jnp.sum(both, axis=0, keepdims=True)
        rsend[slot] = message
        rrecv[slot, me] = message
        for o in others:
            pltpu.make_async_remote_copy(rsend.at[slot], rrecv.at[slot, me], rs.at[slot], rr.at[slot],
                                         device_id=device(*o), device_id_type=MESH).start()

    def wait_rates(slot):
        most = rrecv.at[slot, pl.ds(0, count - 1)]
        pltpu.make_async_copy(most, most, rr.at[slot]).wait()
        pltpu.make_async_copy(most, most, rs.at[slot]).wait()
        total = jnp.sum(rrecv[slot], axis=0)
        first = lax.broadcasted_iota(jnp.int32, (1, lanes), 1) < half
        rate = jnp.sum(jnp.where(first, total, 0.0), axis=1, keepdims=True)
        energy = jnp.sum(jnp.where(first, 0.0, total), axis=1, keepdims=True)
        return rate, energy

    def section(k, p, carry, final):
        fields, energy, clock, table = carry
        q = 1 - p
        if not final:
            set_draws(k + 1, q)
        rate, old = wait_rates(p)
        table = jnp.where((row8 == 0) & (lane8 == k - 1), old / (2.0 * half_sites), table)
        clock = clock + half_sites / rate
        table = jnp.where((row8 == 1) & (lane8 == k), clock, table)
        scaled = rate * (1.0 / half_sites)
        c = scaled * scaled

        def after(s, x):
            xc = x * c
            return s * ((xc - 1.0) / (xc + 1.0))

        energy, own = -fields, zero
        for xi in range(planes):
            s = after(spin[p, xi + 1, body, :], ratio[xi])
            spin[p, xi + 1, body, :] = s
            energy = energy - fold(s * local[xi])
            own = own + fold(s * field[p, xi])
        wait_halo(p)
        if not final:
            gx_, gy_, gz_ = load_ghosts(p)
            nx_, ny_, nz_ = received(p, q)
            store_ghosts(p, after(gx_, nx_), (after(gy_[0], ny_[0]), after(gy_[1], ny_[1])), after(gz_, nz_))
            place_ghosts(p)
            send_rates(q, rates(q), energy)
            send_halo(q, lambda xi: ratio[xi], p)
        return own, energy, clock, table

    pl.semaphore_wait(barrier, count - 1)
    for p in range(2):
        send_halo(2 + p, lambda xi: spin[p, xi + 1, body, :], 1 - p)
    set_draws(0, 0)
    for p in (1, 0):
        wait_halo(2 + p)
        store_ghosts(p, *received(2 + p, 1 - p))
    place_ghosts(1)
    send_rates(0, rates(0), zero)
    send_halo(0, lambda xi: ratio[xi], 1)

    def pair(m, carry):
        carry = section(2 * m, 0, carry, False)
        return section(2 * m + 1, 1, carry, False)

    carry = (field_sum, zero, jnp.zeros((1, 1), jnp.float32), zero)
    carry = lax.fori_loop(0, SECTIONS // 2 - 1, pair, carry)
    carry = section(SECTIONS - 2, 0, carry, False)
    _, energy, _, table = section(SECTIONS - 1, 1, carry, True)
    send_rates(0, zero, energy)

    def finish(xi, none):
        flip = ((row + xi) & 1) == 1
        e, o = spin[0, xi + 1, body, :], spin[1, xi + 1, body, :]
        evens, odds = jnp.where(flip, o, e), jnp.where(flip, e, o)
        out[xi] = exact(jnp.where(low, evens, turn(odds, half)), join)
        out[xi + planes] = exact(jnp.where(low, turn(evens, half), odds), join)
        return none

    lax.fori_loop(0, planes, finish, 0)
    _, old = wait_rates(0)
    table = jnp.where((row8 == 0) & (lane8 == SECTIONS - 1), old / (2.0 * half_sites), table)
    hist[...] = table[0:2, 0:SECTIONS]


def solution(mesh):
    sizes = tuple(mesh.shape[axis] for axis in AXES)

    def step(occupancy, site_field, attempt_rate, uniforms):
        nx, ny, nz = occupancy.shape
        planes = nx // 2
        tiles = ny // 8
        assert nx % 4 == 0 and ny % 8 == 0 and nz % 128 == 0 and planes * tiles <= nz // 2
        xdirs = 1 if sizes[0] == 2 else 2
        count = sizes[0] * sizes[1] * sizes[2]
        vmem = functools.partial(pl.BlockSpec, memory_space=pltpu.VMEM)
        f32 = jnp.float32
        return pl.pallas_call(
            functools.partial(kernel, sizes),
            out_shape=(jax.ShapeDtypeStruct((nx, ny, nz), f32), jax.ShapeDtypeStruct((2, SECTIONS), f32)),
            in_specs=[vmem()] * 4,
            out_specs=(vmem(), vmem()),
            scratch_shapes=[
                pltpu.VMEM((2, planes + 2, ny + 2 * PAD, nz), f32),
                pltpu.VMEM((2, planes, ny, nz), f32),
                pltpu.VMEM((2, planes, ny, nz), f32),
                pltpu.VMEM((2, planes, ny, nz), f32),
                pltpu.VMEM((planes, ny, nz), f32),
                pltpu.VMEM((planes, ny, nz), f32),
                pltpu.VMEM((planes, ny, nz), f32),
                pltpu.VMEM((2, tiles + 3, 8, nz), f32),
                pltpu.VMEM((4, tiles + 3, 8, nz), f32),
                pltpu.VMEM((4, tiles * xdirs + 4, 8, nz), f32),
                pltpu.VMEM((2, 1, nz), f32),
                pltpu.VMEM((2, count, 1, nz), f32),
                pltpu.SemaphoreType.DMA((4,)),
                pltpu.SemaphoreType.DMA((4,)),
                pltpu.SemaphoreType.DMA((2,)),
                pltpu.SemaphoreType.DMA((2,)),
            ],
            compiler_params=pltpu.CompilerParams(collective_id=0, has_side_effects=True),
        )(occupancy, site_field, attempt_rate, uniforms)

    in_specs = (P("gx", "gy", "gz"), P("gx", "gy", "gz"), P("gx", "gy", "gz"), P(None, "gx", "gy", "gz"))
    return jax.shard_map(step, mesh=mesh, in_specs=in_specs, out_specs=(P("gx", "gy", "gz"), P()), check_vma=False)
```

time: 698 us -> 64.2 us (0.09); the launches traced: 686 us -> 64 us
  blocking collectives: 358 us -> 0 us
  other arithmetic: 120 us -> 0 us
  local copies, waits for them, and re-layouts: 98 us -> 3.08 us
  Pallas kernels: 0 us -> 60.3 us
  starting transfers between devices: 56.1 us -> 0 us
  between operations: 27.3 us -> 0.64 us
  waiting for transfers between devices: 26 us -> 0 us
    psum x9 -> x0, blocking collectives: 358 us -> none  [the longest x8 318 us: body(): total_rate = lax.psum(local_rate, ('gx', 'gy', 'gz'))]
    reduce_sum x9 -> x0, other arithmetic: 64 us -> none  [the longest x8 56 us: body(): local_rate = jnp.sum(mask * jnp.exp(rate_log))]
    pallas_call x0 -> x1, Pallas kernels: none -> 60.3 us  [step(): pl.pallas_call(functools.partial(kernel, sizes), out_shape=(jax.ShapeDtyp...]
    ppermute x48 -> x0, starting transfers between devices: 56.1 us -> none  [the longest x24 32 us: padded_2(): after = lax.ppermute(initial, axis, down)]
    unnamed x60 -> x2, local copies, waits for them, and re-layouts: 45.3 us -> 3.08 us
    ppermute x48 -> x0, waiting for transfers between devices: 26 us -> none  [the longest x24 13.8 us: padded_2(): after = lax.ppermute(initial, axis, down)]
    log x8 -> x0, local copies, waits for them, and re-layouts: 23.1 us -> none  [body(): jnp.log(draws_full)]
    concatenate x8 -> x0, local copies, waits for them, and re-layouts: 19.8 us -> none  [padded_2(): shard = jnp.concatenate([before, shard, after], axis=dim)]
  transfers between devices with their start and end apart: 48 -> 0, of which waited for: 14 -> 0; matrix products, arithmetic and copies ran while one was open for 15% -> 0% of each run, Pallas kernels for 0% -> 0%
where the time goes in v1:
time: 64.2 us; the launch traced here: 64 us
  Pallas kernels  60.3 us (94%)
  local copies, waits for them, and re-layouts  3.08 us (5%)
    pallas_call x1, Pallas kernels, step(): pl.pallas_call(functools.partial(kernel, sizes), out_shape=(jax.ShapeDtyp...  60.3 us
    unnamed x2, local copies, waits for them, and re-layouts  3.08 us

profile of v1, /device:TPU:0, one launch (start us, length us, event | category | flops | bytes accessed | tf_op | source)
XLA Modules:
  0.0 64.0 jit_solution(3963737878581164000)
XLA Ops:
  0.6 60.3 %shard_map.59 = (f32[16,64,128]{2,1,0:T(8,128)}, f32[2,8]{1,0:T(2,128)}) custom-call(s32[16,64,128]{2,1,0:T(8,128)} %occ.1, f32[16,64,128]{2,1,0:T(8,128)} %fld.1, f32[16,64,128]{2,1,0:T(8,128)} %att.1, f32[8,16,64,64]{3,2,1,0:T(8,128)} %uni.1), custom_call_target="tpu_custom_call" | custom-call | tf_op jit(solution)/shard_map/pallas_call | solution.py:276
  61.0 1.9 %copy.8 = f32[16,64,128]{2,1,0:T(8,128)} copy(f32[16,64,128]{2,1,0:T(8,128)} %get-tuple-element.4) | data formatting | bytes 1048576
  62.8 1.2 %copy.9 = f32[2,8]{1,0:T(2,128)} copy(f32[2,8]{1,0:T(2,128)} %get-tuple-element.5) | data formatting | bytes 128

commit v2 on v1

--- a/solution.py
+++ b/solution.py
@@ -14,7 +14,7 @@
 PAD = 8
 
 
-def kernel(sizes, occ, fld, att, uni, out, hist, spin, field, rate0, inv, draw, ratio, local, ghost, hsend, hrecv,
+def kernel(sizes, occ_hbm, fld_hbm, att_hbm, uni_hbm, out, hist, occ, fld, att, uni, loaded, spin, field, rate0, inv, draw, ratio, local, ghost, hsend, hrecv,
            rsend, rrecv, hs, hr, rs, rr):
     gx, gy, gz = sizes
     count = gx * gy * gz
@@ -24,6 +24,9 @@
     body = pl.ds(PAD, rows)
     xdirs = 1 if gx == 2 else 2
     ybase, zbase = tiles * xdirs, tiles * xdirs + 2
+    loads = [pltpu.make_async_copy(a, b, loaded.at[i]) for i, (a, b) in enumerate(((occ_hbm, occ), (fld_hbm, fld), (att_hbm, att), (uni_hbm, uni)))]
+    for load in loads:
+        load.start()
     half_sites = float(planes * rows * lanes * count)
     pos = [lax.axis_index(axis) for axis in AXES]
     me = (pos[0] * gy + pos[1]) * gz + pos[2]
@@ -33,7 +36,7 @@
         return (moved[0][dx % gx], moved[1][dy % gy], moved[2][dz % gz])
 
     others = [o for o in itertools.product(range(gx), range(gy), range(gz)) if o != (0, 0, 0)]
-    others.sort(key=lambda o: -(min(o[0], gx - o[0]) + min(o[1], gy - o[1]) + 2 * min(o[2], gz - o[2])))
+    others.sort(key=lambda o: -(min(o[0], gx - o[0]) + min(o[1], gy - o[1]) + 4 * (o[2] % 2) + 2 * (o[2] > 0)))
 
     barrier = pltpu.get_barrier_semaphore()
     for o in others:
@@ -63,67 +66,83 @@
     def exact(a, b):
         return jnp.dot(a, b, precision=lax.Precision.HIGHEST, preferred_element_type=jnp.float32)
 
-    def packed(ref, xi):
-        first = exact(ref[xi].astype(jnp.float32), split)
-        second = exact(ref[xi + planes].astype(jnp.float32), split)
-        evens = jnp.where(low, first, turn(second, half))
-        odds = jnp.where(low, turn(first, half), second)
-        flip = ((row + xi) & 1) == 1
-        return jnp.where(flip, odds, evens), jnp.where(flip, evens, odds)
-
-    def prepare(xi, sums):
-        s = packed(occ, xi)
-        f = packed(fld, xi)
-        a = packed(att, xi)
-        for p in range(2):
-            spin[p, xi + 1, body, :] = 2.0 * s[p] - 1.0
-            field[p, xi] = f[p]
-            rate0[p, xi] = a[p]
-            inv[p, xi] = 1.0 / a[p]
-        return sums + fold(f[1] * (2.0 * s[1] - 1.0))
+    split16 = split.astype(jnp.bfloat16)
+    split48 = jnp.concatenate([split16] * 3, axis=0)
+
+    def packed(ref, xi, n, whole):
+        both = jnp.concatenate([ref[pl.ds(xi, n)].reshape(n * rows, lanes), ref[pl.ds(xi + planes, n)].reshape(n * rows, lanes)], axis=0)
+        if whole:
+            parts = both.astype(jnp.float32).astype(jnp.bfloat16)
+        else:
+            high = both.astype(jnp.bfloat16)
+            rest = both - high.astype(jnp.float32)
+            middle = rest.astype(jnp.bfloat16)
+            parts = jnp.concatenate([high, middle, (rest - middle.astype(jnp.float32)).astype(jnp.bfloat16)], axis=1)
+        moved = jnp.dot(parts, split16 if whole else split48, preferred_element_type=jnp.float32)
+        for i in range(n):
+            first, second = moved[i * rows:(i + 1) * rows], moved[(n + i) * rows:(n + i + 1) * rows]
+            evens = jnp.where(low, first, turn(second, half))
+            odds = jnp.where(low, turn(first, half), second)
+            flip = ((row + xi + i) & 1) == 1
+            yield xi + i, (jnp.where(flip, odds, evens), jnp.where(flip, evens, odds))
+
+    def prepare_spins(group, none):
+        for xi, s in packed(occ, 2 * group, 2, True):
+            for p in range(2):
+                spin[p, xi + 1, body, :] = 2.0 * s[p] - 1.0
+        return none
+
+    def prepare_rest(group, sums):
+        for xi, f in packed(fld, 2 * group, 2, False):
+            for p in range(2):
+                field[p, xi] = f[p]
+            sums = sums + fold(f[1] * spin[1, xi + 1, body, :])
+        for xi, a in packed(att, 2 * group, 2, False):
+            for p in range(2):
+                rate0[p, xi] = a[p]
+                inv[p, xi] = 1.0 / a[p]
+        return sums
 
     def fold(x):
         return jnp.sum(x.reshape(tiles, 8, lanes), axis=0)
 
     zero = jnp.zeros((8, lanes), jnp.float32)
-    field_sum = lax.fori_loop(0, planes, prepare, zero)
+    loads[0].wait()
+    lax.fori_loop(0, planes // 2, prepare_spins, 0)
 
     def set_draws(k, p):
         for xi in range(planes):
             both = jnp.concatenate([uni[k, xi], uni[k, xi + planes]], axis=1)
             draw[xi] = both * inv[p, xi]
 
-    def halo_copies(slot):
-        src = hsend.at[slot]
-        up_x, down_x = device(1, 0, 0), device(-1, 0, 0)
-        dst = hrecv.at[slot]
-        moves = []
-        if xdirs == 1:
-            moves.append((pl.ds(0, tiles), pl.ds(0, tiles), up_x))
-        else:
-            moves.append((pl.ds(0, tiles), pl.ds(0, tiles), down_x))
-            moves.append((pl.ds(0, tiles), pl.ds(tiles, tiles), up_x))
-        moves.append((pl.ds(tiles, 1), pl.ds(ybase, 1), device(0, -1, 0)))
-        moves.append((pl.ds(tiles + 1, 1), pl.ds(ybase + 1, 1), device(0, 1, 0)))
-        moves.append((pl.ds(tiles + 2, 1), pl.ds(zbase, 1), device(0, 0, 1)))
-        moves.append((pl.ds(tiles + 2, 1), pl.ds(zbase + 1, 1), device(0, 0, -1)))
-        for a, b, target in moves:
-            pltpu.make_async_remote_copy(src.at[a], dst.at[b], hs.at[slot], hr.at[slot], device_id=target, device_id_type=MESH).start()
+    def halo_copy(slot, a, b, n, target):
+        pltpu.make_async_remote_copy(hsend.at[slot, pl.ds(a, n)], hrecv.at[slot, pl.ds(b, n)], hs.at[slot], hr.at[slot],
+                                     device_id=target, device_id_type=MESH).start()
 
     def send_halo(slot, plane, user):
-        hsend[slot, pl.ds(0, tiles)] = jnp.where(low, plane(0), plane(planes - 1)).reshape(tiles, 8, lanes)
         tail = jnp.zeros((rows, lanes), jnp.float32)
         for xi in range(planes):
             full = plane(xi)
-            hsend[slot, tiles, pl.ds(xi, 1), :] = full[0:1]
-            hsend[slot, tiles + 1, pl.ds(xi, 1), :] = full[rows - 1:rows]
             ends = jnp.where(kind(xi + user), full, turn(full, -1))
             tail = tail + jnp.where(place == half - 1 - xi, turn(ends, -xi), 0.0)
         z = tail[0:8]
         for t in range(1, tiles):
             z = z + turn(tail[8 * t:8 * t + 8], -planes * t)
         hsend[slot, tiles + 2] = z
-        halo_copies(slot)
+        halo_copy(slot, tiles + 2, zbase, 1, device(0, 0, 1))
+        halo_copy(slot, tiles + 2, zbase + 1, 1, device(0, 0, -1))
+        hsend[slot, pl.ds(0, tiles)] = jnp.where(low, plane(0), plane(planes - 1)).reshape(tiles, 8, lanes)
+        if xdirs == 1:
+            halo_copy(slot, 0, 0, tiles, device(1, 0, 0))
+        else:
+            halo_copy(slot, 0, 0, tiles, device(-1, 0, 0))
+            halo_copy(slot, 0, tiles, tiles, device(1, 0, 0))
+        for xi in range(planes):
+            full = plane(xi)
+            hsend[slot, tiles, pl.ds(xi, 1), :] = full[0:1]
+            hsend[slot, tiles + 1, pl.ds(xi, 1), :] = full[rows - 1:rows]
+        halo_copy(slot, tiles, ybase, 1, device(0, -1, 0))
+        halo_copy(slot, tiles + 1, ybase + 1, 1, device(0, 1, 0))
 
     def wait_halo(slot):
         whole = hrecv.at[slot]
@@ -229,6 +248,10 @@
     pl.semaphore_wait(barrier, count - 1)
     for p in range(2):
         send_halo(2 + p, lambda xi: spin[p, xi + 1, body, :], 1 - p)
+    for load in loads[1:3]:
+        load.wait()
+    field_sum = lax.fori_loop(0, planes // 2, prepare_rest, zero)
+    loads[3].wait()
     set_draws(0, 0)
     for p in (1, 0):
         wait_halo(2 + p)
@@ -259,6 +282,11 @@
     _, old = wait_rates(0)
     table = jnp.where((row8 == 0) & (lane8 == SECTIONS - 1), old / (2.0 * half_sites), table)
     hist[...] = table[0:2, 0:SECTIONS]
+
+
+def hand_over(spins, table, out, hist):
+    out[...] = spins[...]
+    hist[...] = table[...]
 
 
 def solution(mesh):
@@ -273,12 +301,17 @@
         count = sizes[0] * sizes[1] * sizes[2]
         vmem = functools.partial(pl.BlockSpec, memory_space=pltpu.VMEM)
         f32 = jnp.float32
-        return pl.pallas_call(
+        made = pl.pallas_call(
             functools.partial(kernel, sizes),
             out_shape=(jax.ShapeDtypeStruct((nx, ny, nz), f32), jax.ShapeDtypeStruct((2, SECTIONS), f32)),
-            in_specs=[vmem()] * 4,
+            in_specs=[pl.BlockSpec(memory_space=pl.ANY)] * 4,
             out_specs=(vmem(), vmem()),
             scratch_shapes=[
+                pltpu.VMEM((nx, ny, nz), occupancy.dtype),
+                pltpu.VMEM((nx, ny, nz), f32),
+                pltpu.VMEM((nx, ny, nz), f32),
+                pltpu.VMEM(uniforms.shape, f32),
+                pltpu.SemaphoreType.DMA((4,)),
                 pltpu.VMEM((2, planes + 2, ny + 2 * PAD, nz), f32),
                 pltpu.VMEM((2, planes, ny, nz), f32),
                 pltpu.VMEM((2, planes, ny, nz), f32),
@@ -298,6 +331,12 @@
             ],
             compiler_params=pltpu.CompilerParams(collective_id=0, has_side_effects=True),
         )(occupancy, site_field, attempt_rate, uniforms)
+        return pl.pallas_call(
+            hand_over,
+            out_shape=(jax.ShapeDtypeStruct((nx, ny, nz), f32), jax.ShapeDtypeStruct((2, SECTIONS), f32)),
+            in_specs=[vmem()] * 2,
+            out_specs=(vmem(), vmem()),
+        )(*made)
 
     in_specs = (P("gx", "gy", "gz"), P("gx", "gy", "gz"), P("gx", "gy", "gz"), P(None, "gx", "gy", "gz"))
     return jax.shard_map(step, mesh=mesh, in_specs=in_specs, out_specs=(P("gx", "gy", "gz"), P()), check_vma=False)

time: 64.2 us -> 58.9 us (0.917)
  local copies, waits for them, and re-layouts: 3.08 us -> 0 us
  Pallas kernels: 60.3 us -> 58.1 us
    pallas_call x1, Pallas kernels: 60.3 us -> 56.2 us  [step(): pl.pallas_call(functools.partial(kernel, sizes), out_shape=(jax.ShapeDtyp...]
    unnamed x2 -> x0, local copies, waits for them, and re-layouts: 3.08 us -> none
    pallas_call x0 -> x1, Pallas kernels: none -> 1.87 us  [step(): pl.pallas_call(hand_over, out_shape=(jax.ShapeDtypeStruct((nx, ny, nz), f...]
where the time goes in v2:
time: 58.9 us; the launch traced here: 58.7 us
  Pallas kernels  58.1 us (99%)
  between operations  0.64 us (1%)
    pallas_call x1, Pallas kernels, step(): pl.pallas_call(functools.partial(kernel, sizes), out_shape=(jax.ShapeDtyp...  56.2 us
    pallas_call x1, Pallas kernels, step(): pl.pallas_call(hand_over, out_shape=(jax.ShapeDtypeStruct((nx, ny, nz), f...  1.87 us

profile of v2, /device:TPU:0, one launch (start us, length us, event | category | flops | bytes accessed | tf_op | source)
XLA Modules:
  0.0 58.7 jit_solution(13409562251555418030)
XLA Ops:
  0.6 56.2 %shard_map.59 = (f32[16,64,128]{2,1,0:T(8,128)}, f32[2,8]{1,0:T(2,128)}) custom-call(s32[16,64,128]{2,1,0:T(8,128)} %occ_hbm.1, f32[16,64,128]{2,1,0:T(8,128)} %fld_hbm.1, f32[16,64,128]{2,1,0:T(8,128)} %att_hbm.1, f32[8,16,64,64]{3,2,1,0:T(8,128)} %uni_hbm.1), custom_call_target="tpu_custom_call" | custom-call | tf_op jit(solution)/shard_map/pallas_call | solution.py:304
  56.8 1.9 %shard_map.60 = (f32[16,64,128]{2,1,0:T(8,128)}, f32[2,8]{1,0:T(2,128)}) custom-call(f32[16,64,128]{2,1,0:T(8,128)} %get-tuple-element.4.spins, f32[2,8]{1,0:T(2,128)} %get-tuple-element.5.table), custom_call_target="tpu_custom_call" | custom-call | tf_op jit(solution)/shard_map/pallas_call | solution.py:334

commit v3 on v2

--- a/solution.py
+++ b/solution.py
@@ -246,19 +246,20 @@
         return own, energy, clock, table
 
     pl.semaphore_wait(barrier, count - 1)
-    for p in range(2):
+    for p in (1, 0):
         send_halo(2 + p, lambda xi: spin[p, xi + 1, body, :], 1 - p)
     for load in loads[1:3]:
         load.wait()
     field_sum = lax.fori_loop(0, planes // 2, prepare_rest, zero)
     loads[3].wait()
     set_draws(0, 0)
-    for p in (1, 0):
-        wait_halo(2 + p)
-        store_ghosts(p, *received(2 + p, 1 - p))
+    wait_halo(3)
+    store_ghosts(1, *received(3, 0))
     place_ghosts(1)
     send_rates(0, rates(0), zero)
     send_halo(0, lambda xi: ratio[xi], 1)
+    wait_halo(2)
+    store_ghosts(0, *received(2, 1))
 
     def pair(m, carry):
         carry = section(2 * m, 0, carry, False)
@@ -274,14 +275,17 @@
         flip = ((row + xi) & 1) == 1
         e, o = spin[0, xi + 1, body, :], spin[1, xi + 1, body, :]
         evens, odds = jnp.where(flip, o, e), jnp.where(flip, e, o)
-        out[xi] = exact(jnp.where(low, evens, turn(odds, half)), join)
-        out[xi + planes] = exact(jnp.where(low, turn(evens, half), odds), join)
+        fld[xi] = exact(jnp.where(low, evens, turn(odds, half)), join)
+        fld[xi + planes] = exact(jnp.where(low, turn(evens, half), odds), join)
         return none
 
     lax.fori_loop(0, planes, finish, 0)
+    store = pltpu.make_async_copy(fld, out, loaded.at[0])
+    store.start()
     _, old = wait_rates(0)
     table = jnp.where((row8 == 0) & (lane8 == SECTIONS - 1), old / (2.0 * half_sites), table)
     hist[...] = table[0:2, 0:SECTIONS]
+    store.wait()
 
 
 def hand_over(spins, table, out, hist):
@@ -305,7 +309,7 @@
             functools.partial(kernel, sizes),
             out_shape=(jax.ShapeDtypeStruct((nx, ny, nz), f32), jax.ShapeDtypeStruct((2, SECTIONS), f32)),
             in_specs=[pl.BlockSpec(memory_space=pl.ANY)] * 4,
-            out_specs=(vmem(), vmem()),
+            out_specs=(pl.BlockSpec(memory_space=pl.ANY), vmem()),
             scratch_shapes=[
                 pltpu.VMEM((nx, ny, nz), occupancy.dtype),
                 pltpu.VMEM((nx, ny, nz), f32),

time: 58.9 us -> 58.5 us (level)
  no operation moved by 1% of the time
where the time goes in v3:
time: 58.5 us; the launch traced here: 58.3 us
  Pallas kernels  57.7 us (99%)
  between operations  0.64 us (1%)
    pallas_call x1, Pallas kernels, step(): pl.pallas_call(functools.partial(kernel, sizes), out_shape=(jax.ShapeDtyp...  55.8 us
    pallas_call x1, Pallas kernels, step(): pl.pallas_call(hand_over, out_shape=(jax.ShapeDtypeStruct((nx, ny, nz), f...  1.87 us

profile of v3, /device:TPU:0, one launch (start us, length us, event | category | flops | bytes accessed | tf_op | source)
XLA Modules:
  0.0 58.3 jit_solution(1526018230127273034)
XLA Ops:
  0.6 55.8 %shard_map.59 = (f32[16,64,128]{2,1,0:T(8,128)}, f32[2,8]{1,0:T(2,128)}) custom-call(s32[16,64,128]{2,1,0:T(8,128)} %occ_hbm.1, f32[16,64,128]{2,1,0:T(8,128)} %fld_hbm.1, f32[16,64,128]{2,1,0:T(8,128)} %att_hbm.1, f32[8,16,64,64]{3,2,1,0:T(8,128)} %uni_hbm.1), custom_call_target="tpu_custom_call" | custom-call | tf_op jit(solution)/shard_map/pallas_call | solution.py:308
  56.4 1.9 %shard_map.60 = (f32[16,64,128]{2,1,0:T(8,128)}, f32[2,8]{1,0:T(2,128)}) custom-call(f32[16,64,128]{2,1,0:T(8,128)} %get-tuple-element.4.spins, f32[2,8]{1,0:T(2,128)} %get-tuple-element.5.table), custom_call_target="tpu_custom_call" | custom-call | tf_op jit(solution)/shard_map/pallas_call | solution.py:338
